TPU v7x, 64 devices: a 2x2x8 block of a 4x4x8 slice. The times are simulated.
64 devices in a mesh: dp: 8 (over x, y, core), tp: 8 (over z).
Axes of the slice: x: 2, y: 2, z: 8, core: 2. Of those that a mesh axis runs over, the one named last changes fastest.
The devices are a block of a 4x4x8 slice.
Arguments:
- x: bfloat16 [512, 4096], P('dp'), parts along dimension 0
- k_cache: bfloat16 [512, 2048, 8, 128], P('dp', None, 'tp'), parts along dimension 0
- v_cache: bfloat16 [512, 2048, 8, 128], P('dp', None, 'tp'), parts along dimension 0
- gain_a: bfloat16 [4096], replicated
- wq: bfloat16 [4096, 4096], P(None, 'tp')
- wo: bfloat16 [4096, 4096], P('tp')
- gain_m: bfloat16 [4096], replicated
- w_gate: bfloat16 [4096, 12288], P(None, 'tp')
- w_up: bfloat16 [4096, 12288], P(None, 'tp')
- w_down: bfloat16 [12288, 4096], P('tp')
Outputs:
- output: bfloat16 [512, 4096], P('dp'), parts along dimension 0
There are 8 independent parts. A program takes and returns all parts, laid end to end along the dimension named above; an argument that names none is the same for every part.
All inputs are finite; a program needn't handle non-finite values.
Results may differ from a plain program's by a relative error of at most 0.017.
Values are sent between devices in bfloat16 or wider.
A program may use at most 768 MiB of HBM per device.

v0:
```python
import jax
import jax.numpy as jnp
from jax import lax
from jax.sharding import PartitionSpec as P

HEAD = 128
THETA = 10000


def normed(x, gain):
    wide = x.astype(jnp.float32)
    scale = lax.rsqrt(jnp.mean(wide * wide, -1, keepdims=True) + 1e-6)
    return (wide * scale * gain.astype(jnp.float32)).astype(jnp.bfloat16)


def turned(t, place, theta):
    half = t.shape[-1] // 2
    angle = place.astype(jnp.float32)[:, None] * theta ** (-jnp.arange(half, dtype=jnp.float32) / half)
    cos, sin = jnp.cos(angle)[:, None], jnp.sin(angle)[:, None]
    a, b = t[..., :half].astype(jnp.float32), t[..., half:].astype(jnp.float32)
    return jnp.concatenate([a * cos - b * sin, b * cos + a * sin], -1).astype(jnp.bfloat16)


def matmul(a, w):
    return jnp.dot(a, w, preferred_element_type=jnp.float32).astype(jnp.bfloat16)


def einsum(form, a, b):
    return jnp.einsum(form, a.astype(jnp.float32), b.astype(jnp.float32))


def seen_by(a, wq, k_cache, v_cache, head, theta):
    batch, cache, kv_heads = k_cache.shape[:3]
    place = jnp.full((batch,), cache - 1)
    q = turned(matmul(a, wq).reshape(batch, -1, head), place, theta).reshape(batch, kv_heads, -1, head)
    scores = einsum("bgsd,bugd->bgsu", q, k_cache) * head**-0.5
    weights = jax.nn.softmax(scores, -1).astype(jnp.bfloat16)
    return einsum("bgsu,bugd->bgsd", weights, v_cache).astype(jnp.bfloat16).reshape(batch, -1)


def hidden_of(b, w_gate, w_up):
    gate = jnp.dot(b, w_gate, preferred_element_type=jnp.float32)
    up = jnp.dot(b, w_up, preferred_element_type=jnp.float32)
    return (jax.nn.silu(gate) * up).astype(jnp.bfloat16)


def solution(mesh):
    def added(t, term):
        return (t.astype(jnp.float32) + lax.psum(term.astype(jnp.bfloat16), "tp").astype(jnp.float32)).astype(jnp.bfloat16)

    def step(x, k_cache, v_cache, gain_a, wq, wo, gain_m, w_gate, w_up, w_down):
        seen = seen_by(normed(x, gain_a), wq, k_cache, v_cache, HEAD, THETA)
        h = added(x, jnp.dot(seen, wo, preferred_element_type=jnp.float32))
        return added(h, jnp.dot(hidden_of(normed(h, gain_m), w_gate, w_up), w_down, preferred_element_type=jnp.float32))

    states, cache, columns, rows_of = P("dp", None), P("dp", None, "tp", None), P(None, "tp"), P("tp", None)
    return jax.shard_map(
        step,
        mesh=mesh,
        in_specs=(states, cache, cache, P(None), columns, rows_of, P(None), columns, columns, rows_of),
        out_specs=states,
        check_vma=False,
    )
```

profile of v0, /device:TPU:22, one launch (start us, length us, event | category | flops | bytes accessed | tf_op | source)
XLA Modules:
  0.0 209.1 jit_solution(15309871697710427923)
XLA Ops:
  6.5 0.0 all-reduce.3.cloned.1.call-start
  6.6 0.7 convert_element_type.66
  7.3 1.2 fusion.14
  8.6 3.3 %convolution_convert_fusion.2 = bf16[64,512]{1,0:T(8,128)(2,1)S(1)} fusion(bf16[4096,512]{1,0:T(8,128)(2,1)} %param.14, bf16[64,4096]{1,0:T(8,128)(2,1)} %param.10, f32[4096]{0:T(1024)S(1)} %convert_element_type.66, f32[64]{0:T(128)S(1)} %add_rsqrt_fusion.1), kind=kOutput, calls=%fused_computation.20 | convolution fusion | flops 269516800 | bytes 4800768 | tf_op jit(solution)/shard_map/dot_general | solution.py:25
  11.9 0.1 fusion.47
  12.0 0.1 pad_maximum_fusion
  12.1 14.8 %fusion.48 = (f32[64,4]{1,0:T(8,128)S(1)}, f32[64,4,2048]{2,1,0:T(4,128)S(1)}) fusion(bf16[64,2048,1,128]{3,1,2,0:T(8,128)(2,1)} %param.11, bf16[64,4,128]{2,0,1:T(8,128)(2,1)S(1)} %pad_maximum_fusion), kind=kOutput, calls=%fused_computation.58 | convolution fusion | flops 135792640 | bytes 35718144 | tf_op jit(solution)/shard_map/sub | solution.py:37
  26.9 0.0 copy-start.1
  26.9 0.0 copy-start.2
  26.9 0.0 copy-start
  27.0 13.1 %fusion.11 = bf16[64,4,128]{2,1,0:T(4,128)(2,1)S(1)} fusion(bf16[64,2048,1,128]{3,1,2,0:T(8,128)(2,1)} %param.12, f32[64,4,2048]{2,1,0:T(4,128)S(1)} %get-tuple-element.12, f32[64,4]{1,0:T(8,128)S(1)} %get-tuple-element.11), kind=kOutput, calls=%fused_computation.19 | convolution fusion | flops 135299072 | bytes 35718144 | tf_op jit(solution)/shard_map/bgsu,bugd->bgsd/dot_general | solution.py:29
  40.0 0.0 copy-done.1
  40.0 1.6 convolution_convert_fusion
  41.7 0.1 all-reduce.3.cloned.1.call-update
  41.7 0.1 all-reduce.5.cloned.1.call-start
  41.8 0.0 copy-done.2
  41.8 70.9 %all-reduce.3.cloned.1.call-done = bf16[64,4096]{1,0:T(8,128)(2,1)} async-done(((bf16[64,4096]{1,0:T(8,128)(2,1)}), bf16[64,4096]{1,0:T(8,128)(2,1)}) %all-reduce.3.cloned.1.call-update) | async-done | bytes 524304 | tf_op jit(solution)/shard_map/psum | solution.py:49
  112.8 0.0 copy-done
  112.8 1.3 fusion.18
  114.1 6.9 %fusion.34 = f32[64,1536]{1,0:T(8,128)S(1)} fusion(bf16[4096,1536]{1,0:T(8,128)(2,1)} %param.17, bf16[64,4096]{1,0:T(8,128)(2,1)S(1)} %get-tuple-element.6, f32[4096]{0:T(1024)S(1)} %convert_element_type.77, f32[64]{0:T(128)S(1)} %add_rsqrt_fusion), kind=kOutput, calls=%fused_computation.42 | convolution fusion | flops 806354944 | bytes 13517056 | tf_op jit(solution)/shard_map/dot_general | solution.py:42
  121.1 13.5 %convolution_convert_fusion.1 = bf16[64,4096]{1,0:T(8,128)(2,1)} fusion(bf16[1536,4096]{1,0:T(8,128)(2,1)} %param.19, bf16[4096,1536]{1,0:T(8,128)(2,1)} %param.18, f32[64,1536]{1,0:T(8,128)S(1)} %fusion.34, bf16[64,4096]{1,0:T(8,128)(2,1)S(1)} %get-tuple-element.6, f32[4096]{0:T(1024)S(1)} %convert_element_type.77, f32[64]{0:T(128)S(1)} %add_rsqrt_fusion), kind=kOutput, calls=%fused_computation.6 | convolution fusion | flops 1612513280 | bytes 26624256 | tf_op jit(solution)/shard_map/dot_general | solution.py:54
  134.6 0.1 all-reduce.5.cloned.1.call-update
  134.6 65.6 %all-reduce.5.cloned.1.call-done = bf16[64,4096]{1,0:T(8,128)(2,1)} async-done(((bf16[64,4096]{1,0:T(8,128)(2,1)}), bf16[64,4096]{1,0:T(8,128)(2,1)}) %all-reduce.5.cloned.1.call-update) | async-done | bytes 524304 | tf_op jit(solution)/shard_map/psum | solution.py:49
  200.3 2.0 fusion.21
  (6 shorter events, 0.1 us)
Async XLA Ops:
  6.5 106.2 %all-reduce.3.cloned.1.call-start = ((), (), s32[]{:S(2)}) async-start(), calls=%async_computation | async-start | bytes 1048576 | tf_op jit(solution)/shard_map/psum | solution.py:49
  26.9 13.1 %copy-start.1 = (bf16[512,4096]{1,0:T(8,128)(2,1)S(1)}, bf16[512,4096]{1,0:T(8,128)(2,1)}, u32[]{:S(2)}) copy-start(bf16[512,4096]{1,0:T(8,128)(2,1)} %param.15) | copy-start | bytes 12582916
  26.9 14.9 %copy-start.2 = (bf16[4096]{0:T(1024)(128)(2,1)S(1)}, bf16[4096]{0:T(1024)(128)(2,1)}, u32[]{:S(2)}) copy-start(bf16[4096]{0:T(1024)(128)(2,1)} %param.16) | copy-start | bytes 24580
  26.9 85.8 %copy-start = (bf16[64,4096]{1,0:T(8,128)(2,1)S(1)}, bf16[64,4096]{1,0:T(8,128)(2,1)}, u32[]{:S(2)}) copy-start(bf16[64,4096]{1,0:T(8,128)(2,1)} %param.10) | copy-start | bytes 1572868
  41.7 158.5 %all-reduce.5.cloned.1.call-start = ((), (), s32[]{:S(2)}) async-start(), calls=%async_computation.1 | async-start | bytes 1048576 | tf_op jit(solution)/shard_map/psum | solution.py:49
Sparse Core Ops, SparseCore 0:
  41.9 70.8 all-reduce.2
  134.8 65.4 all-reduce.4
where the time goes:
time: 209 us
  waiting for transfers between devices  137 us (66%)
  matrix products  53.2 us (25%)
  between operations  13.5 us (6%)
  other arithmetic  5.44 us (3%)
    psum x2, waiting for transfers between devices, added(): lax.psum(term.astype(jnp.bfloat16), 'tp').astype(jnp.float32)  137 us
    sub x1, matrix products, seen_by(): weights = jax.nn.softmax(scores, -1).astype(jnp.bfloat16)  14.8 us
    dot_general x1, matrix products, step(): jnp.dot(hidden_of(normed(h, gain_m), w_gate, w_up), w_down, preferred_ele...  13.5 us
    dot_general x1, matrix products, einsum(): return jnp.einsum(form, a.astype(jnp.float32), b.astype(jnp.float32))  13.1 us
    dot_general x1, matrix products, hidden_of(): gate = jnp.dot(b, w_gate, preferred_element_type=jnp.float32)  6.94 us
  transfers between devices with their start and end apart: 2, of which 2 were waited for; matrix products, arithmetic and copies ran while one was open for 0% of the time, Pallas kernels for 0%

commit v1 on v0

v1 whole, which is shorter than its diff:
```python
import functools

import jax
import jax.numpy as jnp
import numpy as np
from jax import lax
from jax.experimental import pallas as pl
from jax.experimental.pallas import tpu as pltpu
from jax.sharding import PartitionSpec as P

HEAD = 128
THETA = 10000
GROUPS = 4
RING = 6
CHUNK = 512
F32, BF16 = jnp.float32, jnp.bfloat16


def kernel(n, x_hbm, k_hbm, v_hbm, gains, rope, wq_hbm, wo_hbm, wg_hbm, wu_hbm, wd_hbm, y_ref,
           xs, act, wq, wo, kr, vr, wg, wu, wd, qf, q_left, q_right, os, seen, own1, s1, r1, h_all, hid, s2, r2,
           x_sem, wq_sem, wo_sem, k_sem, v_sem, gu_sem, wd_sem,
           send1, recv1, send2, recv2, send3, recv3, send4, recv4):
    me = lax.axis_index("tp")
    batch, d = xs.shape
    cache = kr.shape[2]
    heads = wq.shape[1] // HEAD
    pairs = batch // 2
    rows = batch // GROUPS
    cols = d // n
    parts = wg.shape[0]

    def peer(o):
        return lax.rem(me + o, n)

    barrier = pltpu.get_barrier_semaphore()
    for o in range(1, n):
        pl.semaphore_signal(barrier, inc=1, device_id={"tp": peer(o)}, device_id_type=pl.DeviceIdType.MESH)

    def k_copy(p, slot):
        return pltpu.make_async_copy(k_hbm.at[pl.ds(2 * p, 2)], kr.at[slot], k_sem.at[slot])

    def v_copy(p, slot):
        return pltpu.make_async_copy(v_hbm.at[pl.ds(2 * p, 2)], vr.at[slot], v_sem.at[slot])

    x_copy = pltpu.make_async_copy(x_hbm, xs, x_sem)
    wq_copy = pltpu.make_async_copy(wq_hbm, wq, wq_sem)
    wo_copy = pltpu.make_async_copy(wo_hbm, wo, wo_sem)
    gu_copies = []
    for c in range(parts):
        at = pl.ds(c * CHUNK, CHUNK)
        gu_copies.append((pltpu.make_async_copy(wg_hbm.at[:, at], wg.at[c], gu_sem.at[2 * c]),
                          pltpu.make_async_copy(wu_hbm.at[:, at], wu.at[c], gu_sem.at[2 * c + 1])))
    order = [o for k in range(n // 2, 0, -1) for o in sorted({k, n - k})] + [0]
    wd_copies = {o: pltpu.make_async_copy(wd_hbm.at[:, pl.ds(pl.multiple_of(peer(o) * cols, cols), cols)], wd.at[o], wd_sem.at[o])
                 for o in order}

    x_copy.start()
    wq_copy.start()
    for p in range(RING):
        k_copy(p, p).start()
        v_copy(p, p).start()
    wo_copy.start()

    x_copy.wait()

    def norm_x(i, _):
        at = pl.ds(pl.multiple_of(i * 16, 16), 16)
        wide = xs[at, :].astype(F32)
        scale = lax.rsqrt(jnp.mean(wide * wide, -1, keepdims=True) + 1e-6)
        act[at, :] = (wide * scale * gains[0:1, :]).astype(BF16)
        return 0

    lax.fori_loop(0, batch // 16, norm_x, 0)

    q_left[...] = jnp.zeros_like(q_left)
    q_right[...] = jnp.zeros_like(q_right)
    wq_copy.wait()
    q = jnp.dot(act[...], wq[...], preferred_element_type=F32).astype(BF16).astype(F32)
    cos, sin = rope[0:1, :], rope[1:2, :]
    for h in range(heads):
        t = q[:, h * HEAD:(h + 1) * HEAD]
        qf[h * batch:(h + 1) * batch, :] = t * cos + pltpu.roll(t, HEAD // 2, 1) * sin
    for h in range(heads):
        for s, side in enumerate((q_left, q_right)):
            side[pl.ds(s * heads + h, pairs, stride=2 * heads), :] = qf[pl.ds(h * batch + s, pairs, stride=2), :]

    first = lax.broadcasted_iota(jnp.int32, (2 * heads, HEAD), 0) < heads

    def attend(p, slot):
        at = pl.ds(pl.multiple_of(p * 2 * heads, 2 * heads), 2 * heads)
        q_pair = jnp.concatenate([q_left[at, :], q_right[at, :]], -1).astype(BF16)
        k_copy(p, slot).wait()
        keys = jnp.concatenate([kr[slot, 0], kr[slot, 1]], -1)
        scores = lax.dot_general(q_pair, keys, (((1,), (1,)), ((), ())), preferred_element_type=F32) * HEAD**-0.5
        e = jnp.exp(scores - jnp.max(scores, -1, keepdims=True))
        weights = (e * (1 / jnp.sum(e, -1, keepdims=True))).astype(BF16)
        v_copy(p, slot).wait()
        values = jnp.concatenate([vr[slot, 0], vr[slot, 1]], -1)
        o = jnp.dot(weights, values, preferred_element_type=F32)
        os[at, :] = jnp.where(first, o[:, :HEAD], o[:, HEAD:]).astype(BF16).astype(F32)

    def rs1(g, o):
        at = pl.ds(g * rows, rows)
        return pltpu.make_async_remote_copy(s1.at[o, at], r1.at[o, at], send1.at[g, o], recv1.at[g, o],
                                            device_id={"tp": peer(o)}, device_id_type=pl.DeviceIdType.MESH)

    def ag1(g, o):
        at = pl.ds(g * rows, rows)
        mine = h_all.at[me, at]
        return pltpu.make_async_remote_copy(mine, mine, send2.at[g, o], recv2.at[g, o],
                                            device_id={"tp": peer(o)}, device_id_type=pl.DeviceIdType.MESH)

    def mine_of(ref, at):
        return ref[at, pl.ds(pl.multiple_of(me * cols, cols), cols)].astype(F32)

    def gather1(g):
        at = slice(g * rows, (g + 1) * rows)
        total = mine_of(xs, at) + own1[at, :]
        for o in range(1, n):
            rs1(g, o).wait_recv()
            total += r1[o, at, :].astype(F32)
        h_all[me, at, :] = total.astype(BF16)
        for o in order[:-1]:
            ag1(g, o).start()

    def norm_h(g):
        at = slice(g * rows, (g + 1) * rows)
        for o in range(1, n):
            ag1(g, o).wait_recv()
        squares = jnp.zeros((rows, 1), F32)
        for j in range(n):
            wide = h_all[j, at, :].astype(F32)
            squares += jnp.sum(wide * wide, -1, keepdims=True)
        scale = lax.rsqrt(squares / d + 1e-6)
        for j in range(n):
            cut = slice(j * cols, (j + 1) * cols)
            act[at, cut] = (h_all[j, at, :].astype(F32) * scale * gains[1:2, cut]).astype(BF16)

    per = pairs // GROUPS
    for g in range(GROUPS):
        def body(i, _):
            for u in range(2):
                p = g * per + 2 * i + u
                slot = lax.rem(p, RING)
                attend(p, slot)

                @pl.when(p + RING < pairs)
                def _():
                    k_copy(p + RING, slot).start()
                    v_copy(p + RING, slot).start()
            return 0

        lax.fori_loop(0, per // 2, body, 0)
        if g == GROUPS - 1:
            pass
        elif g == GROUPS - 2:
            for a, b in gu_copies:
                a.start()
                b.start()
            for o in order:
                wd_copies[o].start()
        at = slice(g * rows, (g + 1) * rows)
        for h in range(heads):
            seen[at, h * HEAD:(h + 1) * HEAD] = os[pl.ds(g * rows * heads + h, rows, stride=heads), :].astype(BF16)
        if g == 0:
            wo_copy.wait()
            pl.semaphore_wait(barrier, n - 1)
        for o in order:
            term = jnp.dot(seen[at, :], wo[:, pl.ds(pl.multiple_of(peer(o) * cols, cols), cols)], preferred_element_type=F32)
            if o:
                s1[o, at, :] = term.astype(BF16)
                rs1(g, o).start()
            else:
                own1[at, :] = term
        if g:
            gather1(g - 1)
        if g > 1:
            norm_h(g - 2)
    gather1(GROUPS - 1)
    norm_h(GROUPS - 2)
    norm_h(GROUPS - 1)

    for c in range(parts):
        gu_copies[c][0].wait()
        gate = jnp.dot(act[...], wg[c], preferred_element_type=F32)
        gu_copies[c][1].wait()
        up = jnp.dot(act[...], wu[c], preferred_element_type=F32)
        hid[:, c * CHUNK:(c + 1) * CHUNK] = (gate * jax.nn.sigmoid(gate) * up).astype(BF16)

    def rs2(o):
        return pltpu.make_async_remote_copy(s2.at[o], r2.at[o], send3.at[o], recv3.at[o],
                                            device_id={"tp": peer(o)}, device_id_type=pl.DeviceIdType.MESH)

    def ag2(o):
        mine = y_ref.at[:, pl.ds(pl.multiple_of(me * cols, cols), cols)]
        return pltpu.make_async_remote_copy(mine, mine, send4.at[o], recv4.at[o],
                                            device_id={"tp": peer(o)}, device_id_type=pl.DeviceIdType.MESH)

    total = None
    for o in order:
        wd_copies[o].wait()
        term = jnp.dot(hid[...], wd[o], preferred_element_type=F32)
        if o:
            s2[o] = term.astype(BF16)
            rs2(o).start()
        else:
            total = term
    total += h_all[me].astype(F32)
    for o in order[:-1][::-1]:
        rs2(o).wait_recv()
        total += r2[o].astype(F32)
    y_ref[:, pl.ds(pl.multiple_of(me * cols, cols), cols)] = total.astype(BF16)
    for o in order[:-1]:
        ag2(o).start()
    for o in range(1, n):
        ag2(o).wait_recv()
    for o in range(1, n):
        for g in range(GROUPS):
            rs1(g, o).wait_send()
            ag1(g, o).wait_send()
        rs2(o).wait_send()
        ag2(o).wait_send()


def solution(mesh):
    n = mesh.shape["tp"]

    def step(x, k_cache, v_cache, gain_a, wq, wo, gain_m, w_gate, w_up, w_down):
        batch, d = x.shape
        cache = k_cache.shape[1]
        ff = w_gate.shape[1]
        heads = wq.shape[1] // HEAD
        cols = d // n
        half = HEAD // 2
        angle = (cache - 1) * np.float64(THETA) ** (-np.arange(half) / half)
        cos, sin = np.cos(angle), np.sin(angle)
        rope = jnp.asarray(np.stack([np.concatenate([cos, cos]), np.concatenate([-sin, sin])]), F32)
        gains = jnp.stack([gain_a, gain_m]).astype(F32)
        vmem, hbm = pl.BlockSpec(memory_space=pltpu.VMEM), pl.BlockSpec(memory_space=pl.ANY)
        dma = pltpu.SemaphoreType.DMA
        parts = ff // CHUNK
        return pl.pallas_call(
            functools.partial(kernel, n),
            out_shape=jax.ShapeDtypeStruct((batch, d), BF16),
            in_specs=[hbm, hbm, hbm, vmem, vmem, hbm, hbm, hbm, hbm, hbm],
            out_specs=vmem,
            scratch_shapes=[
                pltpu.VMEM((batch, d), BF16),
                pltpu.VMEM((batch, d), BF16),
                pltpu.VMEM(wq.shape, BF16),
                pltpu.VMEM(wo.shape, BF16),
                pltpu.VMEM((RING, 2, cache, HEAD), BF16),
                pltpu.VMEM((RING, 2, cache, HEAD), BF16),
                pltpu.VMEM((parts, d, CHUNK), BF16),
                pltpu.VMEM((parts, d, CHUNK), BF16),
                pltpu.VMEM((n, ff, cols), BF16),
                pltpu.VMEM((batch * heads, HEAD), F32),
                pltpu.VMEM((batch * heads, HEAD), F32),
                pltpu.VMEM((batch * heads, HEAD), F32),
                pltpu.VMEM((batch * heads, HEAD), F32),
                pltpu.VMEM((batch, heads * HEAD), BF16),
                pltpu.VMEM((batch, cols), F32),
                pltpu.VMEM((n, batch, cols), BF16),
                pltpu.VMEM((n, batch, cols), BF16),
                pltpu.VMEM((n, batch, cols), BF16),
                pltpu.VMEM((batch, ff), BF16),
                pltpu.VMEM((n, batch, cols), BF16),
                pltpu.VMEM((n, batch, cols), BF16),
                dma, dma, dma, dma((RING,)), dma((RING,)), dma((2 * parts,)), dma((n,)),
                dma((GROUPS, n)), dma((GROUPS, n)), dma((GROUPS, n)), dma((GROUPS, n)), dma((n,)), dma((n,)), dma((n,)), dma((n,)),
            ],
            compiler_params=pltpu.CompilerParams(collective_id=0, has_side_effects=True, vmem_limit_bytes=67043328),
        )(x, k_cache.reshape(batch, cache, HEAD), v_cache.reshape(batch, cache, HEAD), gains, rope, wq, wo, w_gate, w_up, w_down)

    states, cache, columns, rows_of = P("dp", None), P("dp", None, "tp", None), P(None, "tp"), P("tp", None)
    return jax.shard_map(
        step,
        mesh=mesh,
        in_specs=(states, cache, cache, P(None), columns, rows_of, P(None), columns, columns, rows_of),
        out_specs=states,
        check_vma=False,
    )
```

time: 209 us -> 108 us (0.52)
  waiting for transfers between devices: 137 us -> 0 us
  Pallas kernels: 0 us -> 103 us
  matrix products: 53.2 us -> 0 us
  between operations: 13.5 us -> 0.02 us
  other arithmetic: 5.44 us -> 0.66 us
  local copies, waits for them, and re-layouts: 0.14 us -> 3.29 us
    psum x2 -> x0, waiting for transfers between devices: 137 us -> none  [added(): lax.psum(term.astype(jnp.bfloat16), 'tp').astype(jnp.float32)]
    pallas_call x0 -> x1, Pallas kernels: none -> 103 us  [step(): pl.pallas_call(functools.partial(kernel, n), out_shape=jax.ShapeDtypeStru...]
    dot_general x5 -> x0, matrix products: 38.4 us -> none  [the longest x1 13.5 us: step(): jnp.dot(hidden_of(normed(h, gain_m), w_gate, w_up), w_down, preferred_ele...]
    sub x1 -> x0, matrix products: 14.8 us -> none  [seen_by(): weights = jax.nn.softmax(scores, -1).astype(jnp.bfloat16)]
    reduce_sum x2 -> x0, other arithmetic: 2.57 us -> none  [normed(): scale = lax.rsqrt(jnp.mean(wide * wide, -1, keepdims=True) + 1e-06)]
  transfers between devices with their start and end apart: 2 -> 0, of which waited for: 2 -> 0; matrix products, arithmetic and copies ran while one was open for 0% -> 0% of each run, Pallas kernels for 0% -> 0%
where the time goes in v1:
time: 108 us; the launch traced here: 107 us
  Pallas kernels  103 us (95%)
  local copies, waits for them, and re-layouts  3.29 us (3%)
    pallas_call x1, Pallas kernels, step(): pl.pallas_call(functools.partial(kernel, n), out_shape=jax.ShapeDtypeStru...  103 us

profile of v1, /device:TPU:22, one launch (start us, length us, event | category | flops | bytes accessed | tf_op | source)
XLA Modules:
  0.0 106.5 jit_solution(3805716375991715036)
XLA Ops:
  0.0 0.7 stack.9
  0.7 0.7 stack.10
  1.4 0.7 maximum_convert_fusion.gains
  2.1 102.6 %shard_map.109 = bf16[64,4096]{1,0:T(8,128)(2,1)} custom-call(bf16[64,4096]{1,0:T(8,128)(2,1)} %x_hbm.1, bf16[64,2048,128]{2,1,0:T(8,128)(2,1)} %bitcast.2, bf16[64,2048,128]{2,1,0:T(8,128)(2,1)} %bitcast.3, f32[2,4096]{1,0:T(2,128)} %maximum_convert_fusion.gains, f32[2,128]{1,0:T(2,128)} %constant.2.clone.rope, bf16[4096,512]{1,0:T(8,128)(2,1)} %wq_hbm.1, ...), custom_call_target="tpu_custom_call" | custom-call | tf_op jit(solution)/shard_map/pallas_call | solution.py:242
  104.7 1.9 %copy.13 = bf16[64,4096]{1,0:T(8,128)(2,1)} copy(bf16[64,4096]{1,0:T(8,128)(2,1)} %shard_map.109) | data formatting | bytes 1048576

commit v2 on v1

v2 whole, which is shorter than its diff:
```python
import functools

import jax
import jax.numpy as jnp
import numpy as np
from jax import lax
from jax.experimental import pallas as pl
from jax.experimental.pallas import tpu as pltpu
from jax.sharding import PartitionSpec as P

HEAD = 128
THETA = 10000
GROUPS = 4
HALVES = 2
QUAD = 4
RING = 3
CHUNK = 512
F32, BF16 = jnp.float32, jnp.bfloat16


def kernel(n, x_hbm, k_hbm, v_hbm, gains, rope, wq_hbm, wo_hbm, wg_hbm, wu_hbm, wd_hbm, y_hbm,
           xs, act, wq, wo, kr, vr, wg, wu, wd, qf, q_left, q_right, wts, os, seen, t1, s1, r1, h_all, hid, t2, s2, rin, rout, fin, ys,
           x_sem, wq_sem, wo_sem, k_sem, v_sem, gu_sem, wd_sem, y_sem,
           send1, recv1, send2, recv2, send3, recv3, send4, recv4):
    me = lax.axis_index("tp")
    batch, d = xs.shape
    heads = wq.shape[1] // HEAD
    quads = batch // QUAD
    pairs = batch // 2
    rows = batch // GROUPS
    cols = d // n
    half = cols // 2
    parts = wg.shape[0]

    def peer(o):
        return lax.rem(me + o, n)

    def remote(src, dst, send, recv, o):
        return pltpu.make_async_remote_copy(src, dst, send, recv, device_id={"tp": peer(o)}, device_id_type=pl.DeviceIdType.MESH)

    def columns(o, start=0, size=cols):
        return pl.ds(pl.multiple_of(peer(o) * cols + start, half), size)

    barrier = pltpu.get_barrier_semaphore()
    for o in range(1, n):
        pl.semaphore_signal(barrier, inc=1, device_id={"tp": peer(o)}, device_id_type=pl.DeviceIdType.MESH)

    def k_copy(i):
        slot = lax.rem(i, RING)
        return pltpu.make_async_copy(k_hbm.at[pl.ds(QUAD * i, QUAD)], kr.at[slot], k_sem.at[slot])

    def v_copy(i):
        slot = lax.rem(i, RING)
        return pltpu.make_async_copy(v_hbm.at[pl.ds(QUAD * i, QUAD)], vr.at[slot], v_sem.at[slot])

    x_copy = pltpu.make_async_copy(x_hbm, xs, x_sem)
    wq_copy = pltpu.make_async_copy(wq_hbm, wq, wq_sem)
    wo_copy = pltpu.make_async_copy(wo_hbm, wo, wo_sem)
    gu_copies = []
    for c in range(parts):
        at = pl.ds(c * CHUNK, CHUNK)
        gu_copies.append((pltpu.make_async_copy(wg_hbm.at[:, at], wg.at[c], gu_sem.at[2 * c]),
                          pltpu.make_async_copy(wu_hbm.at[:, at], wu.at[c], gu_sem.at[2 * c + 1])))
    order = (4, 3, 5, 2, 6, 1, 7, 0)
    wd_copies = {o: pltpu.make_async_copy(wd_hbm.at[:, columns(o)], wd.at[o], wd_sem.at[o]) for o in order}

    x_copy.start()
    wq_copy.start()
    for i in range(RING):
        k_copy(i).start()
        v_copy(i).start()
    wo_copy.start()

    x_copy.wait()

    def norm_x(i, _):
        at = pl.ds(pl.multiple_of(i * 16, 16), 16)
        wide = xs[at, :].astype(F32)
        scale = lax.rsqrt(jnp.mean(wide * wide, -1, keepdims=True) + 1e-6)
        act[at, :] = (wide * scale * gains[0:1, :]).astype(BF16)
        return 0

    lax.fori_loop(0, batch // 16, norm_x, 0)

    q_left[...] = jnp.zeros_like(q_left)
    q_right[...] = jnp.zeros_like(q_right)
    wq_copy.wait()
    q = jnp.dot(act[...], wq[...], preferred_element_type=F32).astype(BF16).astype(F32)
    cos, sin = rope[0:1, :], rope[1:2, :]
    for h in range(heads):
        t = q[:, h * HEAD:(h + 1) * HEAD]
        qf[h * batch:(h + 1) * batch, :] = t * cos + pltpu.roll(t, HEAD // 2, 1) * sin
    for h in range(heads):
        for s, side in enumerate((q_left, q_right)):
            side[pl.ds(s * heads + h, pairs, stride=2 * heads), :] = qf[pl.ds(h * batch + s, pairs, stride=2), :]

    first = lax.broadcasted_iota(jnp.int32, (2 * heads, HEAD), 0) < heads

    def rows_of(i, u):
        return pl.ds(pl.multiple_of((i * QUAD + 2 * u) * heads, 2 * heads), 2 * heads)

    def scores_of(i, u):
        at, slot = rows_of(i, u), lax.rem(i, RING)
        q_pair = jnp.concatenate([q_left[at, :], q_right[at, :]], -1).astype(BF16)
        keys = jnp.concatenate([kr[slot, 2 * u], kr[slot, 2 * u + 1]], -1)
        return lax.dot_general(q_pair, keys, (((1,), (1,)), ((), ())), preferred_element_type=F32) * HEAD**-0.5

    def softmax(u, scores):
        e = jnp.exp(scores - jnp.max(scores, -1, keepdims=True))
        wts[u] = (e * (1 / jnp.sum(e, -1, keepdims=True))).astype(BF16)

    def values_of(i, u, weights):
        slot = lax.rem(i, RING)
        values = jnp.concatenate([vr[slot, 2 * u], vr[slot, 2 * u + 1]], -1)
        o = jnp.dot(weights, values, preferred_element_type=F32)
        os[rows_of(i, u), :] = jnp.where(first, o[:, :HEAD], o[:, HEAD:]).astype(BF16).astype(F32)

    def attend(i):
        k_copy(i).wait()
        v_copy(i - 1).wait()
        before = [wts[u] for u in range(QUAD // 2)]
        scores = [scores_of(i, u) for u in range(QUAD // 2)]
        for u in range(QUAD // 2):
            values_of(i - 1, u, before[u])
        for u in range(QUAD // 2):
            softmax(u, scores[u])

        @pl.when(i + RING < quads)
        def _():
            k_copy(i + RING).start()

        @pl.when(i - 1 + RING < quads)
        def _():
            v_copy(i - 1 + RING).start()

    def rs1(g, o):
        at = pl.ds(g * rows, rows)
        return remote(s1.at[at, columns(o)], r1.at[o, at], send1.at[g, o], recv1.at[g, o], o)

    def ag1(g, o):
        mine = h_all.at[me, pl.ds(g * rows, rows)]
        return remote(mine, mine, send2.at[g, o], recv2.at[g, o], o)

    def project(g):
        at = slice(g * rows, (g + 1) * rows)
        for h in range(heads):
            seen[at, h * HEAD:(h + 1) * HEAD] = os[pl.ds(g * rows * heads + h, rows, stride=heads), :].astype(BF16)
        term = jnp.dot(seen[at, :], wo[...], preferred_element_type=F32)
        t1[at, :] = term
        s1[at, :] = term.astype(BF16)
        for o in order[:-1]:
            rs1(g, o).start()

    def gather1(g):
        at = slice(g * rows, (g + 1) * rows)
        for o in order[:-1]:
            rs1(g, o).wait_recv()
        total = xs[at, columns(0)].astype(F32) + t1[at, columns(0)]
        for o in range(1, n):
            total += r1[o, at, :].astype(F32)
        h_all[me, at, :] = total.astype(BF16)
        for o in order[:-1]:
            ag1(g, o).start()

    def norm_h(g):
        at = slice(g * rows, (g + 1) * rows)
        for o in range(1, n):
            ag1(g, o).wait_recv()
        squares = jnp.zeros((rows, 1), F32)
        for j in range(n):
            wide = h_all[j, at, :].astype(F32)
            squares += jnp.sum(wide * wide, -1, keepdims=True)
        scale = lax.rsqrt(squares / d + 1e-6)
        for j in range(n):
            cut = slice(j * cols, (j + 1) * cols)
            act[at, cut] = (h_all[j, at, :].astype(F32) * scale * gains[1:2, cut]).astype(BF16)

    k_copy(0).wait()
    for u in range(QUAD // 2):
        softmax(u, scores_of(0, u))
    k_copy(RING).start()

    per = quads // GROUPS
    for g in range(GROUPS):
        last = g == GROUPS - 1

        def body(i, _):
            attend(i)
            return 0

        lax.fori_loop(g * per + 1, (g + 1) * per + 1 - last, body, 0)
        if g == GROUPS - 2:
            for a, b in gu_copies:
                a.start()
                b.start()
            for o in order:
                wd_copies[o].start()
        if last:
            v_copy(quads - 1).wait()
            for u in range(QUAD // 2):
                values_of(quads - 1, u, wts[u])
        if g == 0:
            wo_copy.wait()
            pl.semaphore_wait(barrier, n - 1)
        project(g)
        if g:
            gather1(g - 1)
        if g > 1:
            norm_h(g - 2)

    tall = batch // HALVES

    def gate_up(a, c):
        at = slice(a * tall, (a + 1) * tall)
        if a == 0:
            gu_copies[c][0].wait()
            gu_copies[c][1].wait()
        gate = jnp.dot(act[at, :], wg[c], preferred_element_type=F32)
        up = jnp.dot(act[at, :], wu[c], preferred_element_type=F32)
        hid[at, c * CHUNK:(c + 1) * CHUNK] = (gate * jax.nn.sigmoid(gate) * up).astype(BF16)

    left, right = pl.ds(0, half), pl.ds(half, half)

    def rs2(a, k):
        at = pl.ds(a * tall, tall)
        src, dst, o = (
            (s2.at[3, at], rin.at[0, at], 1),
            (s2.at[5, at], rin.at[1, at], 7),
            (s2.at[4, at, left], rin.at[2, at, left], 2),
            (s2.at[4, at, right], rin.at[2, at, right], 6),
            (s2.at[1, at], fin.at[0, at], 1),
            (s2.at[7, at], fin.at[1, at], 7),
            (rout.at[0, at], fin.at[2, at], 2),
            (rout.at[1, at], fin.at[3, at], 6),
        )[k]
        return remote(src, dst, send3.at[a, k], recv3.at[a, k], o)

    def ag2(a, k):
        at = pl.ds(a * tall, tall)
        where, o = (
            (columns(0), 1),
            (columns(0), 7),
            (columns(0), 2),
            (columns(0), 6),
            (columns(6), 1),
            (columns(2), 7),
            (columns(6, 0, half), 2),
            (columns(2, half, half), 6),
        )[k]
        return remote(ys.at[at, where], ys.at[at, where], send4.at[a, k], recv4.at[a, k], o)

    def down(a, which):
        at = slice(a * tall, (a + 1) * tall)
        if a == 0:
            for o in which:
                wd_copies[o].wait()
        for o in which:
            term = jnp.dot(hid[at, :], wd[o], preferred_element_type=F32)
            if o in (0, 2, 6):
                t2[(0, 2, 6).index(o), at, :] = term
            else:
                s2[o, at, :] = term.astype(BF16)

    def down_all(a):
        down(a, (4, 3, 5))
        for k in range(4):
            rs2(a, k).start()
        down(a, (2, 6, 1, 7))
        rs2(a, 4).start()
        rs2(a, 5).start()
        down(a, (0,))

    def relay2(a):
        at = slice(a * tall, (a + 1) * tall)
        for k in range(4):
            rs2(a, k).wait_recv()
        for side, cut, rest in ((0, slice(0, half), slice(half, cols)), (1, slice(half, cols), slice(0, half))):
            rout[side, at, cut] = (t2[1 + side, at, cut] + rin[side, at, cut].astype(F32) + rin[2, at, cut].astype(F32)).astype(BF16)
            rout[side, at, rest] = (t2[1 + side, at, rest] + rin[side, at, rest].astype(F32)).astype(BF16)
        rs2(a, 6).start()
        rs2(a, 7).start()

    def finish(a):
        at = slice(a * tall, (a + 1) * tall)
        for k in range(4, 8):
            rs2(a, k).wait_recv()
        total = h_all[me, at, :].astype(F32) + t2[0, at, :]
        for k in range(4):
            total += fin[k, at, :].astype(F32)
        ys[at, columns(0)] = total.astype(BF16)
        for k in range(4):
            ag2(a, k).start()

    def hand_on(a):
        ag2(a, 2).wait_recv()
        ag2(a, 4).start()
        ag2(a, 6).start()
        ag2(a, 3).wait_recv()
        ag2(a, 5).start()
        ag2(a, 7).start()

    def y_copy(a):
        at = pl.ds(a * tall, tall)
        return pltpu.make_async_copy(ys.at[at], y_hbm.at[at], y_sem.at[a])

    def out(a):
        for k in (0, 1, 4, 5, 6, 7):
            ag2(a, k).wait_recv()
        for k in range(4, 8):
            ag2(a, k).wait_send()
        y_copy(a).start()

    gate_up(0, 0)
    gather1(GROUPS - 1)
    norm_h(GROUPS - 2)
    for c in range(1, parts):
        gate_up(0, c)
    down_all(0)
    norm_h(GROUPS - 1)
    gate_up(1, 0)
    relay2(0)
    gate_up(1, 1)
    finish(0)
    gate_up(1, 2)
    hand_on(0)
    down_all(1)
    out(0)
    relay2(1)
    finish(1)
    hand_on(1)
    out(1)
    for a in range(HALVES):
        y_copy(a).wait()
        for k in range(8):
            rs2(a, k).wait_send()
        for k in range(4):
            ag2(a, k).wait_send()
    for o in range(1, n):
        for g in range(GROUPS):
            rs1(g, o).wait_send()
            ag1(g, o).wait_send()


def solution(mesh):
    n = mesh.shape["tp"]

    def step(x, k_cache, v_cache, gain_a, wq, wo, gain_m, w_gate, w_up, w_down):
        batch, d = x.shape
        cache = k_cache.shape[1]
        ff = w_gate.shape[1]
        heads = wq.shape[1] // HEAD
        cols = d // n
        half = HEAD // 2
        angle = (cache - 1) * np.float64(THETA) ** (-np.arange(half) / half)
        cos, sin = np.cos(angle), np.sin(angle)
        rope = jnp.asarray(np.stack([np.concatenate([cos, cos]), np.concatenate([-sin, sin])]), F32)
        gains = jnp.stack([gain_a, gain_m]).astype(F32)
        vmem, hbm = pl.BlockSpec(memory_space=pltpu.VMEM), pl.BlockSpec(memory_space=pl.ANY)
        dma = pltpu.SemaphoreType.DMA
        parts = ff // CHUNK
        return pl.pallas_call(
            functools.partial(kernel, n),
            out_shape=jax.ShapeDtypeStruct((batch, d), BF16),
            in_specs=[hbm, hbm, hbm, vmem, vmem, hbm, hbm, hbm, hbm, hbm],
            out_specs=hbm,
            scratch_shapes=[
                pltpu.VMEM((batch, d), BF16),
                pltpu.VMEM((batch, d), BF16),
                pltpu.VMEM(wq.shape, BF16),
                pltpu.VMEM(wo.shape, BF16),
                pltpu.VMEM((RING, QUAD, cache, HEAD), BF16),
                pltpu.VMEM((RING, QUAD, cache, HEAD), BF16),
                pltpu.VMEM((parts, d, CHUNK), BF16),
                pltpu.VMEM((parts, d, CHUNK), BF16),
                pltpu.VMEM((n, ff, cols), BF16),
                pltpu.VMEM((batch * heads, HEAD), F32),
                pltpu.VMEM((batch * heads, HEAD), F32),
                pltpu.VMEM((batch * heads, HEAD), F32),
                pltpu.VMEM((QUAD // 2, 2 * heads, cache), BF16),
                pltpu.VMEM((batch * heads, HEAD), F32),
                pltpu.VMEM((batch, heads * HEAD), BF16),
                pltpu.VMEM((batch, d), F32),
                pltpu.VMEM((batch, d), BF16),
                pltpu.VMEM((n, batch, cols), BF16),
                pltpu.VMEM((n, batch, cols), BF16),
                pltpu.VMEM((batch, ff), BF16),
                pltpu.VMEM((3, batch, cols), F32),
                pltpu.VMEM((n, batch, cols), BF16),
                pltpu.VMEM((3, batch, cols), BF16),
                pltpu.VMEM((2, batch, cols), BF16),
                pltpu.VMEM((4, batch, cols), BF16),
                pltpu.VMEM((batch, d), BF16),
                dma, dma, dma, dma((RING,)), dma((RING,)), dma((2 * parts,)), dma((n,)), dma((HALVES,)),
                dma((GROUPS, n)), dma((GROUPS, n)), dma((GROUPS, n)), dma((GROUPS, n)),
                dma((HALVES, 8)), dma((HALVES, 8)), dma((HALVES, 8)), dma((HALVES, 8)),
            ],
            compiler_params=pltpu.CompilerParams(collective_id=0, has_side_effects=True, vmem_limit_bytes=67043328),
        )(x, k_cache.reshape(batch, cache, HEAD), v_cache.reshape(batch, cache, HEAD), gains, rope, wq, wo, w_gate, w_up, w_down)

    states, cache, columns, rows_of = P("dp", None), P("dp", None, "tp", None), P(None, "tp"), P("tp", None)
    return jax.shard_map(
        step,
        mesh=mesh,
        in_specs=(states, cache, cache, P(None), columns, rows_of, P(None), columns, columns, rows_of),
        out_specs=states,
        check_vma=False,
    )
```

time: 108 us -> 93.7 us (0.87)
  Pallas kernels: 103 us -> 89.3 us
    pallas_call x1, Pallas kernels: 103 us -> 89.3 us  [step(): pl.pallas_call(functools.partial(kernel, n), out_shape=jax.ShapeDtypeStru...]
where the time goes in v2:
time: 93.7 us; the launch traced here: 93.3 us
  Pallas kernels  89.3 us (95%)
  local copies, waits for them, and re-layouts  3.29 us (4%)
    pallas_call x1, Pallas kernels, step(): pl.pallas_call(functools.partial(kernel, n), out_shape=jax.ShapeDtypeStru...  89.3 us

profile of v2, /device:TPU:22, one launch (start us, length us, event | category | flops | bytes accessed | tf_op | source)
XLA Modules:
  0.0 93.3 jit_solution(16926035073110798961)
XLA Ops:
  0.0 0.7 stack.9
  0.7 0.7 stack.10
  1.4 0.7 maximum_convert_fusion.gains
  2.1 89.3 %shard_map.109 = bf16[64,4096]{1,0:T(8,128)(2,1)} custom-call(bf16[64,4096]{1,0:T(8,128)(2,1)} %x_hbm.1, bf16[64,2048,128]{2,1,0:T(8,128)(2,1)} %bitcast.2, bf16[64,2048,128]{2,1,0:T(8,128)(2,1)} %bitcast.3, f32[2,4096]{1,0:T(2,128)} %maximum_convert_fusion.gains, f32[2,128]{1,0:T(2,128)} %constant.2.clone.rope, bf16[4096,512]{1,0:T(8,128)(2,1)} %wq_hbm.1, ...), custom_call_target="tpu_custom_call" | custom-call | tf_op jit(solution)/shard_map/pallas_call | solution.py:361
  91.4 1.9 %copy.13 = bf16[64,4096]{1,0:T(8,128)(2,1)} copy(bf16[64,4096]{1,0:T(8,128)(2,1)} %shard_map.109) | data formatting | bytes 1048576

commit v3 on v2

--- a/solution.py
+++ b/solution.py
@@ -18,9 +18,9 @@
 F32, BF16 = jnp.float32, jnp.bfloat16
 
 
-def kernel(n, x_hbm, k_hbm, v_hbm, gains, rope, wq_hbm, wo_hbm, wg_hbm, wu_hbm, wd_hbm, y_hbm,
-           xs, act, wq, wo, kr, vr, wg, wu, wd, qf, q_left, q_right, wts, os, seen, t1, s1, r1, h_all, hid, t2, s2, rin, rout, fin, ys,
-           x_sem, wq_sem, wo_sem, k_sem, v_sem, gu_sem, wd_sem, y_sem,
+def kernel(n, x_hbm, k_hbm, v_hbm, ga_hbm, gm_hbm, rope_hbm, wq_hbm, wo_hbm, wg_hbm, wu_hbm, wd_hbm, ys,
+           xs, act, packed, gains, rope, wq, wo, ring, wg, wu, qf, q_left, q_right, wts, os, seen, t1, s1, r1, h_all, hid, t2, s2, rin, rout, fin,
+           x_sem, g_sem, wq_sem, wo_sem, k_sem, v_sem, gu_sem, wd_sem,
            send1, recv1, send2, recv2, send3, recv3, send4, recv4):
     me = lax.axis_index("tp")
     batch, d = xs.shape
@@ -31,6 +31,8 @@
     cols = d // n
     half = cols // 2
     parts = wg.shape[0]
+    cache = k_hbm.shape[1]
+    depth = wd_hbm.shape[0]
 
     def peer(o):
         return lax.rem(me + o, n)
@@ -45,13 +47,28 @@
     for o in range(1, n):
         pl.semaphore_signal(barrier, inc=1, device_id={"tp": peer(o)}, device_id_type=pl.DeviceIdType.MESH)
 
-    def k_copy(i):
-        slot = lax.rem(i, RING)
-        return pltpu.make_async_copy(k_hbm.at[pl.ds(QUAD * i, QUAD)], kr.at[slot], k_sem.at[slot])
-
-    def v_copy(i):
-        slot = lax.rem(i, RING)
-        return pltpu.make_async_copy(v_hbm.at[pl.ds(QUAD * i, QUAD)], vr.at[slot], v_sem.at[slot])
+    def place(i, of_values):
+        return pl.ds(pl.multiple_of((lax.rem(i, RING) + RING * of_values) * cache, cache), cache)
+
+    def kv_copies(i, hbm, sems, of_values):
+        return [pltpu.make_async_copy(hbm.at[QUAD * i + u], ring.at[place(i, of_values), pl.ds(u * HEAD, HEAD)], sems.at[lax.rem(i, RING), u])
+                for u in range(QUAD)]
+
+    def k_start(i):
+        for copy in kv_copies(i, k_hbm, k_sem, 0):
+            copy.start()
+
+    def v_start(i):
+        for copy in kv_copies(i, v_hbm, v_sem, 1):
+            copy.start()
+
+    def k_wait(i):
+        for copy in kv_copies(i, k_hbm, k_sem, 0):
+            copy.wait()
+
+    def v_wait(i):
+        for copy in kv_copies(i, v_hbm, v_sem, 1):
+            copy.wait()
 
     x_copy = pltpu.make_async_copy(x_hbm, xs, x_sem)
     wq_copy = pltpu.make_async_copy(wq_hbm, wq, wq_sem)
@@ -62,22 +79,33 @@
         gu_copies.append((pltpu.make_async_copy(wg_hbm.at[:, at], wg.at[c], gu_sem.at[2 * c]),
                           pltpu.make_async_copy(wu_hbm.at[:, at], wu.at[c], gu_sem.at[2 * c + 1])))
     order = (4, 3, 5, 2, 6, 1, 7, 0)
-    wd_copies = {o: pltpu.make_async_copy(wd_hbm.at[:, columns(o)], wd.at[o], wd_sem.at[o]) for o in order}
+    wd_at = {o: pl.ds(k * depth, depth) for k, o in enumerate(order)}
+    wd_copies = {o: pltpu.make_async_copy(wd_hbm.at[:, columns(o)], ring.at[wd_at[o]], wd_sem.at[o]) for o in order}
+    small = [pltpu.make_async_copy(ga_hbm, packed.at[0], g_sem.at[0]), pltpu.make_async_copy(gm_hbm, packed.at[1], g_sem.at[1]),
+             pltpu.make_async_copy(rope_hbm, rope, g_sem.at[2])]
 
     x_copy.start()
+    for copy in small:
+        copy.start()
     wq_copy.start()
+
+    for copy in small:
+        copy.wait()
+    for k in range(2):
+        gains[k] = packed[k].astype(F32)
+    x_copy.wait()
     for i in range(RING):
-        k_copy(i).start()
-        v_copy(i).start()
+        k_start(i)
+        v_start(i)
     wo_copy.start()
-
-    x_copy.wait()
 
     def norm_x(i, _):
         at = pl.ds(pl.multiple_of(i * 16, 16), 16)
         wide = xs[at, :].astype(F32)
         scale = lax.rsqrt(jnp.mean(wide * wide, -1, keepdims=True) + 1e-6)
-        act[at, :] = (wide * scale * gains[0:1, :]).astype(BF16)
+        for j in range(d // HEAD):
+            cut = slice(j * HEAD, (j + 1) * HEAD)
+            act[at, cut] = (wide[:, cut] * scale * gains[0, j:j + 1, :]).astype(BF16)
         return 0
 
     lax.fori_loop(0, batch // 16, norm_x, 0)
@@ -100,9 +128,9 @@
         return pl.ds(pl.multiple_of((i * QUAD + 2 * u) * heads, 2 * heads), 2 * heads)
 
     def scores_of(i, u):
-        at, slot = rows_of(i, u), lax.rem(i, RING)
+        at = rows_of(i, u)
         q_pair = jnp.concatenate([q_left[at, :], q_right[at, :]], -1).astype(BF16)
-        keys = jnp.concatenate([kr[slot, 2 * u], kr[slot, 2 * u + 1]], -1)
+        keys = ring[place(i, 0), 2 * u * HEAD:(2 * u + 2) * HEAD]
         return lax.dot_general(q_pair, keys, (((1,), (1,)), ((), ())), preferred_element_type=F32) * HEAD**-0.5
 
     def softmax(u, scores):
@@ -110,14 +138,13 @@
         wts[u] = (e * (1 / jnp.sum(e, -1, keepdims=True))).astype(BF16)
 
     def values_of(i, u, weights):
-        slot = lax.rem(i, RING)
-        values = jnp.concatenate([vr[slot, 2 * u], vr[slot, 2 * u + 1]], -1)
+        values = ring[place(i, 1), 2 * u * HEAD:(2 * u + 2) * HEAD]
         o = jnp.dot(weights, values, preferred_element_type=F32)
         os[rows_of(i, u), :] = jnp.where(first, o[:, :HEAD], o[:, HEAD:]).astype(BF16).astype(F32)
 
     def attend(i):
-        k_copy(i).wait()
-        v_copy(i - 1).wait()
+        k_wait(i)
+        v_wait(i - 1)
         before = [wts[u] for u in range(QUAD // 2)]
         scores = [scores_of(i, u) for u in range(QUAD // 2)]
         for u in range(QUAD // 2):
@@ -127,11 +154,11 @@
 
         @pl.when(i + RING < quads)
         def _():
-            k_copy(i + RING).start()
+            k_start(i + RING)
 
         @pl.when(i - 1 + RING < quads)
         def _():
-            v_copy(i - 1 + RING).start()
+            v_start(i - 1 + RING)
 
     def rs1(g, o):
         at = pl.ds(g * rows, rows)
@@ -171,14 +198,14 @@
             wide = h_all[j, at, :].astype(F32)
             squares += jnp.sum(wide * wide, -1, keepdims=True)
         scale = lax.rsqrt(squares / d + 1e-6)
-        for j in range(n):
-            cut = slice(j * cols, (j + 1) * cols)
-            act[at, cut] = (h_all[j, at, :].astype(F32) * scale * gains[1:2, cut]).astype(BF16)
-
-    k_copy(0).wait()
+        for j in range(d // HEAD):
+            lanes = slice(j * HEAD % cols, j * HEAD % cols + HEAD)
+            act[at, j * HEAD:(j + 1) * HEAD] = (h_all[j * HEAD // cols, at, lanes].astype(F32) * scale * gains[1, j:j + 1, :]).astype(BF16)
+
+    k_wait(0)
     for u in range(QUAD // 2):
         softmax(u, scores_of(0, u))
-    k_copy(RING).start()
+    k_start(RING)
 
     per = quads // GROUPS
     for g in range(GROUPS):
@@ -186,27 +213,33 @@
 
         def body(i, _):
             attend(i)
+            if last:
+
+                @pl.when(i == quads - RING)
+                def _():
+                    for a, b in gu_copies:
+                        a.start()
+                        b.start()
+
             return 0
 
-        lax.fori_loop(g * per + 1, (g + 1) * per + 1 - last, body, 0)
-        if g == GROUPS - 2:
-            for a, b in gu_copies:
-                a.start()
-                b.start()
+        with jax.named_scope(f"attend{g}"):
+            lax.fori_loop(g * per + 1, (g + 1) * per + 1 - last, body, 0)
+        if last:
+            v_wait(quads - 1)
+            for u in range(QUAD // 2):
+                values_of(quads - 1, u, wts[u])
             for o in order:
                 wd_copies[o].start()
-        if last:
-            v_copy(quads - 1).wait()
-            for u in range(QUAD // 2):
-                values_of(quads - 1, u, wts[u])
         if g == 0:
-            wo_copy.wait()
-            pl.semaphore_wait(barrier, n - 1)
-        project(g)
+            with jax.named_scope("barrier"):
+                wo_copy.wait()
+                pl.semaphore_wait(barrier, n - 1)
+        with jax.named_scope(f"project{g}"):
+            project(g)
         if g:
-            gather1(g - 1)
-        if g > 1:
-            norm_h(g - 2)
+            with jax.named_scope(f"gather{g - 1}"):
+                gather1(g - 1)
 
     tall = batch // HALVES
 
@@ -255,7 +288,7 @@
             for o in which:
                 wd_copies[o].wait()
         for o in which:
-            term = jnp.dot(hid[at, :], wd[o], preferred_element_type=F32)
+            term = jnp.dot(hid[at, :], ring[wd_at[o], :], preferred_element_type=F32)
             if o in (0, 2, 6):
                 t2[(0, 2, 6).index(o), at, :] = term
             else:
@@ -265,10 +298,9 @@
         down(a, (4, 3, 5))
         for k in range(4):
             rs2(a, k).start()
-        down(a, (2, 6, 1, 7))
+        down(a, (2, 6, 1, 7, 0))
         rs2(a, 4).start()
         rs2(a, 5).start()
-        down(a, (0,))
 
     def relay2(a):
         at = slice(a * tall, (a + 1) * tall)
@@ -299,41 +331,38 @@
         ag2(a, 5).start()
         ag2(a, 7).start()
 
-    def y_copy(a):
-        at = pl.ds(a * tall, tall)
-        return pltpu.make_async_copy(ys.at[at], y_hbm.at[at], y_sem.at[a])
-
     def out(a):
         for k in (0, 1, 4, 5, 6, 7):
             ag2(a, k).wait_recv()
-        for k in range(4, 8):
-            ag2(a, k).wait_send()
-        y_copy(a).start()
-
-    gate_up(0, 0)
-    gather1(GROUPS - 1)
-    norm_h(GROUPS - 2)
-    for c in range(1, parts):
-        gate_up(0, c)
-    down_all(0)
-    norm_h(GROUPS - 1)
-    gate_up(1, 0)
-    relay2(0)
-    gate_up(1, 1)
-    finish(0)
-    gate_up(1, 2)
-    hand_on(0)
-    down_all(1)
-    out(0)
-    relay2(1)
-    finish(1)
-    hand_on(1)
-    out(1)
+
+    def step(do, *args):
+        with jax.named_scope("_".join([do.__name__, *map(str, args)])):
+            do(*args)
+
+    step(norm_h, 0)
+    step(norm_h, 1)
+    step(gate_up, 0, 0)
+    step(gather1, 3)
+    step(gate_up, 0, 1)
+    step(gate_up, 0, 2)
+    step(norm_h, 2)
+    step(down_all, 0)
+    step(norm_h, 3)
+    step(relay2, 0)
+    with jax.named_scope("gate_up_1"):
+        for c in range(parts):
+            gate_up(1, c)
+    step(finish, 0)
+    step(down_all, 1)
+    step(hand_on, 0)
+    step(relay2, 1)
+    step(finish, 1)
+    step(out, 0)
+    step(hand_on, 1)
+    step(out, 1)
     for a in range(HALVES):
-        y_copy(a).wait()
         for k in range(8):
             rs2(a, k).wait_send()
-        for k in range(4):
             ag2(a, k).wait_send()
     for o in range(1, n):
         for g in range(GROUPS):
@@ -354,25 +383,25 @@
         angle = (cache - 1) * np.float64(THETA) ** (-np.arange(half) / half)
         cos, sin = np.cos(angle), np.sin(angle)
         rope = jnp.asarray(np.stack([np.concatenate([cos, cos]), np.concatenate([-sin, sin])]), F32)
-        gains = jnp.stack([gain_a, gain_m]).astype(F32)
         vmem, hbm = pl.BlockSpec(memory_space=pltpu.VMEM), pl.BlockSpec(memory_space=pl.ANY)
         dma = pltpu.SemaphoreType.DMA
         parts = ff // CHUNK
         return pl.pallas_call(
             functools.partial(kernel, n),
-            out_shape=jax.ShapeDtypeStruct((batch, d), BF16),
-            in_specs=[hbm, hbm, hbm, vmem, vmem, hbm, hbm, hbm, hbm, hbm],
-            out_specs=hbm,
+            out_shape=pltpu.VMEM((batch, d), BF16),
+            in_specs=[hbm] * 11,
+            out_specs=vmem,
             scratch_shapes=[
                 pltpu.VMEM((batch, d), BF16),
                 pltpu.VMEM((batch, d), BF16),
+                pltpu.VMEM((2, d // HEAD, HEAD), BF16),
+                pltpu.VMEM((2, d // HEAD, HEAD), F32),
+                pltpu.VMEM(rope.shape, F32),
                 pltpu.VMEM(wq.shape, BF16),
                 pltpu.VMEM(wo.shape, BF16),
-                pltpu.VMEM((RING, QUAD, cache, HEAD), BF16),
-                pltpu.VMEM((RING, QUAD, cache, HEAD), BF16),
+                pltpu.VMEM((2 * RING * cache, QUAD * HEAD), BF16),
                 pltpu.VMEM((parts, d, CHUNK), BF16),
                 pltpu.VMEM((parts, d, CHUNK), BF16),
-                pltpu.VMEM((n, ff, cols), BF16),
                 pltpu.VMEM((batch * heads, HEAD), F32),
                 pltpu.VMEM((batch * heads, HEAD), F32),
                 pltpu.VMEM((batch * heads, HEAD), F32),
@@ -389,13 +418,12 @@
                 pltpu.VMEM((3, batch, cols), BF16),
                 pltpu.VMEM((2, batch, cols), BF16),
                 pltpu.VMEM((4, batch, cols), BF16),
-                pltpu.VMEM((batch, d), BF16),
-                dma, dma, dma, dma((RING,)), dma((RING,)), dma((2 * parts,)), dma((n,)), dma((HALVES,)),
+                dma, dma((3,)), dma, dma, dma((RING, QUAD)), dma((RING, QUAD)), dma((2 * parts,)), dma((n,)),
                 dma((GROUPS, n)), dma((GROUPS, n)), dma((GROUPS, n)), dma((GROUPS, n)),
                 dma((HALVES, 8)), dma((HALVES, 8)), dma((HALVES, 8)), dma((HALVES, 8)),
             ],
-            compiler_params=pltpu.CompilerParams(collective_id=0, has_side_effects=True, vmem_limit_bytes=67043328),
-        )(x, k_cache.reshape(batch, cache, HEAD), v_cache.reshape(batch, cache, HEAD), gains, rope, wq, wo, w_gate, w_up, w_down)
+            compiler_params=pltpu.CompilerParams(collective_id=0, has_side_effects=True, vmem_limit_bytes=56 << 20),
+        )(x, k_cache.reshape(batch, cache, HEAD), v_cache.reshape(batch, cache, HEAD), gain_a.reshape(-1, HEAD), gain_m.reshape(-1, HEAD), rope, wq, wo, w_gate, w_up, w_down)
 
     states, cache, columns, rows_of = P("dp", None), P("dp", None, "tp", None), P(None, "tp"), P("tp", None)
     return jax.shard_map(

time: 93.7 us -> 77.6 us (0.83)
  Pallas kernels: 89.3 us -> 76.6 us
  local copies, waits for them, and re-layouts: 3.29 us -> 0.8 us
    pallas_call x1, Pallas kernels: 89.3 us -> 76.6 us  [step(): pl.pallas_call(functools.partial(kernel, n), out_shape=pltpu.VMEM((batch,...]
    another operation x2 -> x0, local copies, waits for them, and re-layouts: 1.42 us -> none  [step(): gains = jnp.stack([gain_a, gain_m]).astype(F32)]
    unnamed x1, local copies, waits for them, and re-layouts: 1.87 us -> 0.8 us
where the time goes in v3:
time: 77.6 us; the launch traced here: 77.4 us
  Pallas kernels  76.6 us (99%)
  local copies, waits for them, and re-layouts  0.8 us (1%)
    pallas_call x1, Pallas kernels, step(): pl.pallas_call(functools.partial(kernel, n), out_shape=pltpu.VMEM((batch,...  76.6 us

profile of v3, /device:TPU:22, one launch (start us, length us, event | category | flops | bytes accessed | tf_op | source)
XLA Modules:
  0.0 77.4 jit_solution(10253264744020595151)
XLA Ops:
  0.0 76.6 %shard_map.109 = bf16[64,4096]{1,0:T(8,128)(2,1)S(1)} custom-call(bf16[64,4096]{1,0:T(8,128)(2,1)} %x_hbm.1, bf16[64,2048,128]{2,1,0:T(8,128)(2,1)} %bitcast.4, bf16[64,2048,128]{2,1,0:T(8,128)(2,1)} %bitcast.5, bf16[32,128]{1,0:T(8,128)(2,1)} %bitcast.6, bf16[32,128]{1,0:T(8,128)(2,1)} %bitcast.7, f32[2,128]{1,0:T(2,128)} %constant.2.clone.rope_hbm, ...), custom_call_target="tpu_custom_call" | custom-call | tf_op jit(solution)/shard_map/pallas_call | solution.py:389
  76.6 0.8 %copy.13 = bf16[64,4096]{1,0:T(8,128)(2,1)} copy(bf16[64,4096]{1,0:T(8,128)(2,1)S(1)} %shard_map.109) | data formatting | bytes 1048576
